TPU v7x, 512 devices: a whole 4x8x8 slice. The times are simulated.
512 devices in a mesh: dev: 512 (over z, y, x, core).
Axes of the slice: x: 4, y: 8, z: 8, core: 2. Of those that a mesh axis runs over, the one named last changes fastest.
Arguments:
- image_feats: bfloat16 [6144, 1152], P('dev'), may hold values from -0.1875 to 0.1875
- text_feats: bfloat16 [6144, 1152], P('dev'), may hold values from -0.1875 to 0.1875
- image_head: bfloat16 [1152, 640], replicated, may hold values from -0.1875 to 0.1875
- text_head: bfloat16 [1152, 640], replicated, may hold values from -0.1875 to 0.1875
- log_scale: float32 [], replicated, may hold values from 1.6 to 2.3
- logit_bias: float32 [], replicated, may hold values from -8 to -4
- image_group: int32 [6144], P('dev'), may hold values from 0 to 3071
- text_group: int32 [6144], P('dev'), may hold values from 0 to 3071
Outputs:
- loss: float32 [], replicated
- grad_images: bfloat16 [6144, 1152], P('dev')
- grad_texts: bfloat16 [6144, 1152], P('dev')
- grad_scale: float32 [], replicated
- grad_bias: float32 [], replicated
All inputs are finite; a program needn't handle non-finite values.
Results may differ from a plain program's by a relative error of at most 0.0063.
Values may be sent and summed in bfloat16 or wider, within the bound.
A program may use at most 128 MiB of HBM per device.

v0:
```python
import jax
import jax.numpy as jnp
from jax import lax
from jax.sharding import Mesh
from jax.sharding import PartitionSpec as P

DEV = ("dev_0", "dev_1", "dev_2", "dev_3")


epsilon = 1e-06


def one_axis_at_a_time(x, axes):
    for axis in axes:
        x = lax.psum(x, axis)
    return x


def normalize(projected):
    length = jnp.sqrt(jnp.sum(projected * projected, axis=1, keepdims=True) + epsilon)
    return (projected / length, length)


def backward_rows(grad_unit, unit_vec, length, weights):
    inner = jnp.sum(unit_vec * grad_unit, axis=1, keepdims=True)
    grad_proj = ((grad_unit - unit_vec * inner) / length).astype(jnp.bfloat16)
    result = lax.dot_general(
        grad_proj, weights, (((1,), (1,)), ((), ())), preferred_element_type=jnp.float32
    )
    return result.astype(jnp.bfloat16)


def on_device(
    image_feats, text_feats, image_head, text_head, log_scale, logit_bias, image_group, text_group
):
    img_unit, img_length = normalize(
        jnp.dot(image_feats, image_head, preferred_element_type=jnp.float32)
    )
    txt_unit, txt_length = normalize(
        jnp.dot(text_feats, text_head, preferred_element_type=jnp.float32)
    )
    img_emb = img_unit.astype(jnp.bfloat16)
    txt_emb = txt_unit.astype(jnp.bfloat16)
    logit_scale = jnp.exp(log_scale)
    pairs = image_feats.shape[0] * lax.axis_size(DEV)
    stacked_emb = jnp.stack([img_emb, txt_emb])
    stacked_ids = jnp.stack([image_group, text_group])
    emb_piece = lax.all_gather(stacked_emb, DEV, axis=1, tiled=True)
    id_piece = lax.all_gather(stacked_ids, DEV, axis=1, tiled=True)
    cap_emb = emb_piece[1]
    cosine = lax.dot_general(
        img_emb, cap_emb, (((1,), (1,)), ((), ())), preferred_element_type=jnp.float32
    )
    label_sign = jnp.where(image_group[:, None] == id_piece[1][None, :], 1.0, -1.0).astype(
        jnp.float32
    )
    margin = label_sign * (logit_scale * cosine + logit_bias)
    slopes = -label_sign * jax.nn.sigmoid(-margin)
    grad_img = logit_scale * jnp.dot(
        slopes.astype(jnp.bfloat16), cap_emb, preferred_element_type=jnp.float32
    )
    added = jnp.stack(
        [jnp.sum(jax.nn.softplus(-margin)), jnp.sum(slopes * cosine), jnp.sum(slopes)]
    )
    caption_side = (grad_img, added)
    img_piece = emb_piece[0]
    cosine = lax.dot_general(
        img_piece, txt_emb, (((1,), (1,)), ((), ())), preferred_element_type=jnp.float32
    )
    label_sign = jnp.where(id_piece[0][:, None] == text_group[None, :], 1.0, -1.0).astype(
        jnp.float32
    )
    margin = label_sign * (logit_scale * cosine + logit_bias)
    slopes = (-label_sign * jax.nn.sigmoid(-margin)).astype(jnp.bfloat16)
    update = lax.dot_general(
        slopes, img_piece, (((0,), (0,)), ((), ())), preferred_element_type=jnp.float32
    )
    grad_txt = logit_scale * update
    grad_img, local_sums = caption_side
    totals = one_axis_at_a_time(local_sums, DEV)
    loss = totals[0] / pairs
    grad_scale = logit_scale * totals[1] / pairs
    grad_bias = totals[2] / pairs
    grad_images = backward_rows(grad_img, img_unit, img_length, image_head)
    grad_texts = backward_rows(grad_txt, txt_unit, txt_length, text_head)
    return (loss, grad_images, grad_texts, grad_scale, grad_bias)


def solution(mesh):
    torus = Mesh(mesh.devices.reshape(8, 8, 4, 2), ("dev_0", "dev_1", "dev_2", "dev_3"))
    return jax.shard_map(
        on_device,
        mesh=torus,
        in_specs=(P(DEV, None), P(DEV, None), P(), P(), P(), P(), P(DEV), P(DEV)),
        out_specs=(P(), P(DEV, None), P(DEV, None), P(), P()),
        check_vma=False,
    )
```

profile of v0, /device:TPU:1, one launch (start us, length us, event | category | flops | bytes accessed | tf_op | source)
XLA Modules:
  0.0 272.3 jit_solution(15377897066713356984)
XLA Ops:
  7.2 0.0 copy-start
  7.2 0.0 all-gather.3.cloned.1.call-start
  7.2 1.9 multiply_reduce_fusion.4
  9.2 0.0 copy-done
  9.2 1.2 multiply_reduce_fusion.3
  10.4 0.1 convert_bitcast_fusion
  10.5 0.6 copy.17
  11.1 0.0 all-gather.3.cloned.1.call-update
  12.5 0.7 add_bitcast_fusion
  13.2 78.0 %all-gather = s32[512,12,2]{1,2,0:T(2,128)S(1)} all-gather(s32[1,12,2]{1,2,0:T(2,128)S(1)} %add_bitcast_fusion), channel_id=1, replica_groups=mesh['dev_0'=8,'dev_1'=8,'dev_2'=4,'dev_3'=2] {'dev_0','dev_1','dev_2','..., dimensions={0}, use_global_device_ids=true | all-gather | bytes 49248 | tf_op jit(solution)/shard_map/all_gather | solution.py:49
  91.2 0.4 reshape.32
  91.6 0.0 copy-start.3
  91.6 61.6 %all-gather.3.cloned.1.call-done = bf16[2,6144,640]{2,0,1:T(2,128)(2,1)} async-done(((bf16[2,12,640]{2,0,1:T(2,128)(2,1)}), bf16[2,6144,640]{2,0,1:T(2,128)(2,1)}) %all-gather.3.cloned.1.call-update) | async-done | bytes 15728656 | tf_op jit(solution)/shard_map/all_gather | solution.py:48
  153.2 30.7 %fusion.34 = (bf16[1,6144,640]{2,0,1:T(2,128)(2,1)}, bf16[1,6144,640]{2,0,1:T(2,128)(2,1)S(1)}) fusion(bf16[2,6144,640]{2,0,1:T(2,128)(2,1)} %all-gather.3.cloned.1.call-done), kind=kLoop, calls=%fused_computation.57 | loop fusion | bytes 31457280 | tf_op jit(solution)/shard_map/slice | solution.py:66
  183.9 0.0 copy-start.1
  183.9 5.5 %copy-done.1 = bf16[1,6144,640]{2,0,1:T(2,128)(2,1)} copy-done((bf16[1,6144,640]{2,0,1:T(2,128)(2,1)}, bf16[1,6144,640]{2,0,1:T(2,128)(2,1)S(1)}, u32[]{:S(2)}) %copy-start.1) | copy-done | bytes 7864344
  189.4 0.0 copy-done.3
  189.4 2.8 %fusion.15 = (f32[]{:T(128)}, f32[]{:T(128)}, f32[]{:T(128)}, f32[12,6144]{1,0:T(8,128)S(1)}) fusion(f32[]{:T(128)S(6)} %copy.45, f32[]{:T(128)S(6)} %exp.13, s32[6144]{0:T(1024)S(1)} %bitcast.53, s32[12]{0:T(128)S(1)} %copy-done.3, bf16[1,6144,640]{2,0,1:T(2,128)(2,1)S(1)} %get-tuple-element.9, f32[12,640]{1,0:T(8,128)S(1)} %get-tuple-element.18, ...), kind=kOutput, calls=%fused_computation.24 | convolution fusion | flops 95861760 | bytes 8214644 | tf_op jit(solution)/shard_map/dot_general | solution.py:51
  192.3 0.0 copy-start.4
  192.3 2.0 pad_maximum_fusion.1
  194.3 11.8 %psum.28 = f32[3]{0:T(128)S(1)} all-reduce(f32[3]{0:T(128)S(1)} %pad_maximum_fusion.1), channel_id=1, replica_groups=mesh['dev_0'=8,'dev_1'=8,'dev_2'=4,'dev_3'=2] {'dev_0'}, use_global_device_ids=true, to_apply=%region_5.6 | all-reduce | flops 3 | bytes 24 | tf_op jit(solution)/shard_map/psum | solution.py:15
  206.1 12.6 %psum.29 = f32[3]{0:T(128)S(1)} all-reduce(f32[3]{0:T(128)S(1)} %psum.28), channel_id=1, replica_groups=mesh['dev_0'=8,'dev_1'=8,'dev_2'=4,'dev_3'=2] {'dev_1'}, use_global_device_ids=true, to_apply=%region_6.7 | all-reduce | flops 3 | bytes 24 | tf_op jit(solution)/shard_map/psum | solution.py:15
  218.7 6.5 %psum.30 = f32[3]{0:T(128)S(1)} all-reduce(f32[3]{0:T(128)S(1)} %psum.29), channel_id=1, replica_groups=mesh['dev_0'=8,'dev_1'=8,'dev_2'=4,'dev_3'=2] {'dev_2'}, use_global_device_ids=true, to_apply=%region_7.8 | all-reduce | flops 3 | bytes 24 | tf_op jit(solution)/shard_map/psum | solution.py:15
  225.3 6.8 %multiply_reduce_fusion.2 = (f32[12]{0:T(128)S(1)}, f32[12,640]{1,0:T(8,128)S(1)}) fusion(f32[12,640]{1,0:T(8,128)S(1)} %get-tuple-element.18, f32[12]{0:T(128)S(1)} %add_sqrt_fusion.1, bf16[1,6144,640]{2,0,1:T(2,128)(2,1)} %copy-done.1, f32[]{:T(128)S(6)} %copy.45, f32[12,6144]{1,0:T(8,128)S(1)} %get-tuple-element.19, f32[]{:T(128)S(6)} %exp.13, ...), kind=kOutput, calls=%fused_computation.37 | convolution fusion | flops 95139824 | bytes 8245400 | tf_op jit(solution)/shard_map/dot_general | solution.py:59
  232.1 11.8 %psum.31 = f32[3]{0:T(128)S(1)} all-reduce(f32[3]{0:T(128)S(1)} %psum.30), channel_id=1, replica_groups=mesh['dev_0'=8,'dev_1'=8,'dev_2'=4,'dev_3'=2] {'dev_3'}, use_global_device_ids=true, to_apply=%region_8.9 | all-reduce | flops 3 | bytes 24 | tf_op jit(solution)/shard_map/psum | solution.py:15
  243.9 0.6 fusion.36
  246.4 0.0 copy-done.4
  246.4 0.0 copy-start.2
  246.4 13.3 %multiply_reduce_fusion.1 = (f32[12]{0:T(128)S(1)}, f32[12,640]{1,0:T(8,128)S(1)}) fusion(f32[12,640]{1,0:T(8,128)S(1)} %get-tuple-element.16, f32[12]{0:T(128)S(1)} %add_sqrt_fusion, bf16[1,6144,640]{2,0,1:T(2,128)(2,1)} %get-tuple-element.8, f32[]{:T(128)S(6)} %copy.45, f32[]{:T(128)S(6)} %exp.13, s32[6144]{0:T(1024)S(1)} %bitcast.52, s32[12]{0:T(128)S(1)} %copy-done.4), kind=kOutput, calls=%fused_computation.35 | convolution fusion | flops 189527024 | bytes 7950488 | tf_op jit(solution)/shard_map/dot_general | solution.py:75
  259.8 1.2 convolution_convert_fusion
  261.0 0.0 copy-done.2
  261.0 1.2 convolution_convert_fusion.1
  (5 shorter events, 0.1 us)
Async XLA Ops:
  7.2 2.0 copy-start
  7.2 146.0 %all-gather.3.cloned.1.call-start = ((), (), s32[]{:S(2)}) async-start(), calls=%async_computation | async-start | bytes 15759360 | tf_op jit(solution)/shard_map/all_gather | solution.py:48
  91.6 97.9 %copy-start.3 = (s32[12]{0:T(128)S(1)}, s32[12]{0:T(128)}, u32[]{:S(2)}) copy-start(s32[12]{0:T(128)} %param.14) | copy-start | bytes 148
  183.9 5.5 %copy-start.1 = (bf16[1,6144,640]{2,0,1:T(2,128)(2,1)}, bf16[1,6144,640]{2,0,1:T(2,128)(2,1)S(1)}, u32[]{:S(2)}) copy-start(bf16[1,6144,640]{2,0,1:T(2,128)(2,1)S(1)} %get-tuple-element.9) | copy-start | bytes 23592964
  192.3 54.2 %copy-start.4 = (s32[12]{0:T(128)S(1)}, s32[12]{0:T(128)}, u32[]{:S(2)}) copy-start(s32[12]{0:T(128)} %param.15) | copy-start | bytes 148
  246.4 14.5 %copy-start.2 = (bf16[1152,640]{1,0:T(8,128)(2,1)S(1)}, bf16[1152,640]{1,0:T(8,128)(2,1)}, u32[]{:S(2)}) copy-start(bf16[1152,640]{1,0:T(8,128)(2,1)} %param.10) | copy-start | bytes 4423684
Sparse Core Ops, SparseCore 0:
  13.2 139.9 all-gather.2
where the time goes:
time: 273 us; the launch traced here: 272 us
  blocking collectives  121 us (44%)
  waiting for transfers between devices  61.6 us (23%)
  local copies, waits for them, and re-layouts  37.9 us (14%)
  matrix products  28.4 us (10%)
  between operations  20.8 us (8%)
  other arithmetic  2.83 us (1%)
    all_gather x1, blocking collectives, on_device(): id_piece = lax.all_gather(stacked_ids, DEV, axis=1, tiled=True)  78 us
    all_gather x1, waiting for transfers between devices, on_device(): emb_piece = lax.all_gather(stacked_emb, DEV, axis=1, tiled=True)  61.6 us
    psum x4, blocking collectives, one_axis_at_a_time(): x = lax.psum(x, axis)  42.8 us
    slice x1, local copies, waits for them, and re-layouts, on_device(): img_piece = emb_piece[0]  30.7 us
    dot_general x1, matrix products, on_device(): lax.dot_general(slopes, img_piece, (((0,), (0,)), ((), ())), preferred_el...  13.3 us
    dot_general x1, matrix products, on_device(): jnp.dot(slopes.astype(jnp.bfloat16), cap_emb, preferred_element_type=jnp....  6.77 us
    unnamed x11, local copies, waits for them, and re-layouts  5.9 us
  transfers between devices with their start and end apart: 1, of which 1 were waited for; matrix products, arithmetic and copies ran while one was open for 0% of the time, Pallas kernels for 0%

commit v1 on v0

v1 whole, which is shorter than its diff:
```python
import functools

import jax
import jax.numpy as jnp
from jax import lax
from jax.experimental import pallas as pl
from jax.experimental.pallas import tpu as pltpu
from jax.sharding import Mesh
from jax.sharding import PartitionSpec as P

DEV = ("dev_0", "dev_1", "dev_2", "dev_3")
RING = 8
ROWS = 12
PAD = 16
D = 1152
E = 640
W = E + 128
PAIRS = 6144
NEAR = (4, 3, 5, 2, 6, 1, 7)

EPS = 1e-6
F32 = jnp.float32
BF16 = jnp.bfloat16


def nt(a, b):
    return lax.dot_general(a, b, (((1,), (1,)), ((), ())), preferred_element_type=F32)


def nn(a, b):
    return lax.dot_general(a, b, (((1,), (0,)), ((), ())), preferred_element_type=F32)


def tn(a, b):
    return lax.dot_general(a, b, (((0,), (0,)), ((), ())), preferred_element_type=F32)


def id_features(ids, image_side):
    shape = (PAD, 128)
    row = lax.broadcasted_iota(jnp.int32, shape, 0)
    lane = lax.broadcasted_iota(jnp.int32, shape, 1)
    value = jnp.zeros(shape, jnp.int32)
    for r in range(ROWS):
        value = jnp.where(row == r, ids[r], value)
    high, low = value >> 6, value & 63
    square = high * high + low * low
    upper = jnp.where(row < ROWS, square >> 6, -192)
    lower = square & 63
    one, many = jnp.ones(shape, jnp.int32), jnp.full(shape, 64, jnp.int32)
    if image_side:
        parts = (high, low, upper, lower, many, one)
    else:
        parts = (-2 * high, -2 * low, many, one, upper, lower)
    out = jnp.zeros(shape, jnp.int32)
    for k, part in enumerate(parts):
        out = jnp.where(lane == k, part, out)
    return out.astype(F32).astype(BF16)


def project(feats, head):
    proj = nn(feats[...], head[...])
    length = jnp.sqrt(jnp.sum(proj * proj, axis=1, keepdims=True) + EPS)
    return proj / length, length


def kernel(
    ifeat, tfeat, ihead_hbm, thead_hbm, log_scale, logit_bias, igroup, tgroup,
    loss_o, gimg_o, gtxt_o, gscale_o, gbias_o,
    ihead, thead, iemb, temb, iown, town, cos_s, dist_s, slope_s, acc_i, acc_t,
    part_i, part_t, core_rx, mid_i, mid_t, x_rx_i, x_rx_t, ring_i, ring_t,
    sums_v, sum_z, sum_y, sum_c,
    head_sem, s_g1i, r_g1i, s_g1t, r_g1t, s_x, r_x, s_core, r_core,
    s_r1i, r_r1i, s_r1t, r_r1t, s_sz, r_sz, s_sy, r_sy, s_sc, r_sc,
):
    z, y, x, c = (lax.axis_index(a) for a in DEV)
    odd = lax.rem(x, 2)
    x_hi = lax.rem(x + 3 + 2 * odd, 4)
    x_lo = x + 1 - 2 * odd
    other = 1 - c

    head_copies = [
        pltpu.make_async_copy(ihead_hbm, ihead, head_sem.at[0]),
        pltpu.make_async_copy(thead_hbm, thead, head_sem.at[1]),
    ]
    for copy in head_copies:
        copy.start()

    rz = [lax.rem(z + k, RING) for k in NEAR]
    ry = [lax.rem(y + k, RING) for k in NEAR]
    cluster = [(lax.rem(x + dx, 4), lax.rem(c + dc, 2)) for dx in range(4) for dc in range(2) if (dx, dc) != (0, 0)]

    barrier = pltpu.get_barrier_semaphore()
    for t in rz:
        pl.semaphore_signal(barrier, inc=1, device_id={"dev_0": t})
    for t in ry:
        pl.semaphore_signal(barrier, inc=1, device_id={"dev_1": t})
    for tx, tc in cluster:
        pl.semaphore_signal(barrier, inc=1, device_id={"dev_2": tx, "dev_3": tc})

    def send(src, dst, ssem, rsem, device):
        copy = pltpu.make_async_remote_copy(src, dst, ssem, rsem, device_id=device)
        copy.start()
        return copy

    sent = []

    iown[...] = jnp.zeros_like(iown)
    town[...] = jnp.zeros_like(town)
    iown[:, E:] = id_features(igroup, True)
    town[:, E:] = id_features(tgroup, False)
    head_copies[0].wait()
    img_unit, img_len = project(ifeat, ihead)
    iown[0:ROWS, 0:E] = img_unit.astype(BF16)
    iemb[0, z] = iown[...]
    pl.semaphore_wait(barrier, 21)
    for k, t in enumerate(rz):
        sent.append(send(iown, iemb.at[0, z], s_g1i.at[k], r_g1i.at[z], {"dev_0": t}))
    head_copies[1].wait()
    txt_unit, txt_len = project(tfeat, thead)
    town[0:ROWS, 0:E] = txt_unit.astype(BF16)
    temb[0, 0, y] = town[...]
    for k, t in enumerate(ry):
        sent.append(send(town, temb.at[0, 0, y], s_g1t.at[k], r_g1t.at[y], {"dev_1": t}))

    def arrived(dst, rsem):
        pltpu.make_async_copy(dst, dst, rsem).wait()

    for t in rz[::-1]:
        arrived(iemb.at[0, t], r_g1i.at[t])
    sent.append(send(iemb.at[0], iemb.at[1], s_x.at[0], r_x.at[0], {"dev_2": x_hi}))
    for t in ry[::-1]:
        arrived(temb.at[0, 0, t], r_g1t.at[t])
    sent.append(send(temb.at[0, 0], temb.at[0, 1], s_x.at[1], r_x.at[1], {"dev_2": x_lo}))
    sent.append(send(temb.at[0, 0], temb.at[1, 0], s_core.at[0], r_core.at[0], {"dev_3": other}))
    arrived(temb.at[0, 1], r_x.at[1])
    sent.append(send(temb.at[0, 1], temb.at[1, 1], s_core.at[1], r_core.at[1], {"dev_3": other}))
    arrived(iemb.at[1], r_x.at[0])

    scale_row = jnp.exp(jnp.full((1, 256), log_scale[0], F32))
    bias = logit_bias[0]
    n_img = 2 * RING * PAD
    images = iemb.at[...]

    def pair_block(h, totals):
        ie = iemb[...].reshape(n_img, W)
        te = temb[h].reshape(n_img, W)
        cos_s[...] = nt(ie[:, :E], te[:, :E])
        dist_s[...] = nt(ie[:, E:], te[:, E:])
        step = 32

        def rows(i, totals):
            at = pl.ds(pl.multiple_of(i * step, step), step)
            cosine = cos_s[at, :]
            dist = dist_s[at, :]
            match = dist < 0.5
            valid = dist > -0.5
            logit = scale_row * cosine + bias
            minus = jnp.where(match, -logit, logit)
            small = jnp.exp(-jnp.abs(minus))
            ratio = 1.0 / (1.0 + small)
            sig = jnp.where(minus >= 0, ratio, small * ratio)
            slope = jnp.where(valid, jnp.where(match, -sig, sig), 0.0)
            soft = jnp.where(valid, jnp.maximum(minus, 0.0) + jnp.log1p(small), 0.0)
            slope_s[at, :] = slope.astype(BF16)
            fold = lambda a: a[0:8] + a[8:16] + a[16:24] + a[24:32]
            return (
                totals[0] + fold(soft),
                totals[1] + fold(slope * cosine),
                totals[2] + fold(slope),
            )

        totals = lax.fori_loop(0, n_img // step, rows, totals)
        slope = slope_s[...]
        grad_i = nn(slope, te[:, :E])
        grad_t = tn(slope, ie[:, :E])
        return grad_i, grad_t, totals

    zero = jnp.zeros((8, 256), F32)
    totals = (zero, zero, zero)
    grad_i, grad_t, totals = pair_block(0, totals)
    acc_i[...] = grad_i
    acc_t[...] = grad_t
    arrived(temb.at[1, 0], r_core.at[0])
    arrived(temb.at[1, 1], r_core.at[1])
    grad_i, grad_t, totals = pair_block(1, totals)
    part_t[...] = grad_t.astype(BF16).reshape(2, RING, PAD, E)
    sent.append(send(part_t, core_rx, s_core.at[2], r_core.at[2], {"dev_3": other}))
    grad_i = (grad_i + acc_i[...]).reshape(2, RING, PAD, E)
    part_i[...] = grad_i[1].astype(BF16)
    acc_i[...] = grad_i.reshape(n_img, E)
    sent.append(send(part_i, x_rx_i, s_x.at[2], r_x.at[2], {"dev_2": x_hi}))

    lanes = [t[:, 0:128] + t[:, 128:256] for t in totals]
    mine = jnp.concatenate([jnp.sum(t, axis=0, keepdims=True) for t in lanes] + [jnp.zeros((5, 128), F32)], axis=0)
    sums_v[0] = mine
    sum_z[z] = mine
    for k, t in enumerate(rz):
        sent.append(send(sums_v.at[0], sum_z.at[z], s_sz.at[k], r_sz.at[z], {"dev_0": t}))

    arrived(core_rx, r_core.at[2])
    grad_t = acc_t[...].reshape(2, RING, PAD, E) + core_rx[...].astype(F32)
    mid_t[...] = grad_t[1].astype(BF16)
    acc_t[0 : RING * PAD] = grad_t[0].reshape(RING * PAD, E)
    sent.append(send(mid_t, x_rx_t, s_x.at[3], r_x.at[3], {"dev_2": x_lo}))

    arrived(x_rx_i, r_x.at[2])
    mid_i[...] = (acc_i[0 : RING * PAD].reshape(RING, PAD, E) + x_rx_i[...].astype(F32)).astype(BF16)
    ring_i[z] = mid_i[z]
    for k, t in enumerate(rz):
        sent.append(send(mid_i.at[t], ring_i.at[z], s_r1i.at[k], r_r1i.at[z], {"dev_0": t}))

    for t in rz:
        arrived(sum_z.at[t], r_sz.at[t])
    mine = functools.reduce(lambda a, b: a + b, [sum_z[k] for k in range(RING)])
    sums_v[1] = mine
    sum_y[y] = mine
    for k, t in enumerate(ry):
        sent.append(send(sums_v.at[1], sum_y.at[y], s_sy.at[k], r_sy.at[y], {"dev_1": t}))

    arrived(x_rx_t, r_x.at[3])
    part_b = acc_t[0 : RING * PAD].reshape(RING, PAD, E) + x_rx_t[...].astype(F32)
    part_t2 = part_b.astype(BF16)
    core_rx[0] = part_t2
    ring_t[y] = core_rx[0, y]
    for k, t in enumerate(ry):
        sent.append(send(core_rx.at[0, t], ring_t.at[y], s_r1t.at[k], r_r1t.at[y], {"dev_1": t}))

    for t in ry:
        arrived(sum_y.at[t], r_sy.at[t])
    mine = functools.reduce(lambda a, b: a + b, [sum_y[k] for k in range(RING)])
    sums_v[2] = mine
    sum_c[2 * x + c] = mine
    for k, (tx, tc) in enumerate(cluster):
        sent.append(send(sums_v.at[2], sum_c.at[2 * x + c], s_sc.at[k], r_sc.at[2 * x + c], {"dev_2": tx, "dev_3": tc}))

    scale_e = jnp.exp(jnp.full((1, E), log_scale[0], F32))

    def backward(ring, unit, length, head, out):
        grad = functools.reduce(lambda a, b: a + b, [ring[k].astype(F32) for k in range(RING)])
        grad = scale_e * grad[0:ROWS]
        inner = jnp.sum(unit * grad, axis=1, keepdims=True)
        low = ((grad - unit * inner) / length).astype(BF16)
        out[...] = nt(low, head[...]).astype(BF16)

    for t in rz[::-1]:
        arrived(ring_i.at[t], r_r1i.at[t])
    backward(ring_i, img_unit, img_len, ihead, gimg_o)
    for t in ry[::-1]:
        arrived(ring_t.at[t], r_r1t.at[t])
    backward(ring_t, txt_unit, txt_len, thead, gtxt_o)

    for tx, tc in cluster:
        arrived(sum_c.at[2 * tx + tc], r_sc.at[2 * tx + tc])
    mine = functools.reduce(lambda a, b: a + b, [sum_c[k] for k in range(8)])
    whole = jnp.sum(mine, axis=1, keepdims=True) / PAIRS
    scale_1 = jnp.exp(jnp.full((1, 1), log_scale[0], F32))
    loss_o[...] = whole[0:1]
    gscale_o[...] = scale_1 * whole[1:2]
    gbias_o[...] = whole[2:3]

    for copy in sent:
        copy.wait_send()


def on_device(ifeat, tfeat, ihead, thead, log_scale, logit_bias, igroup, tgroup):
    vmem = pl.BlockSpec(memory_space=pltpu.VMEM)
    smem = pl.BlockSpec(memory_space=pltpu.SMEM)
    hbm = pl.BlockSpec(memory_space=pl.ANY)
    dma = pltpu.SemaphoreType.DMA
    blocks = RING * PAD
    one = jax.ShapeDtypeStruct((1, 1), F32)
    grad = jax.ShapeDtypeStruct((ROWS, D), BF16)
    loss, gimg, gtxt, gscale, gbias = pl.pallas_call(
        kernel,
        out_shape=(one, grad, grad, one, one),
        in_specs=[vmem, vmem, hbm, hbm, smem, smem, smem, smem],
        out_specs=[vmem] * 5,
        scratch_shapes=[
            pltpu.VMEM((D, E), BF16),
            pltpu.VMEM((D, E), BF16),
            pltpu.VMEM((2, RING, PAD, W), BF16),
            pltpu.VMEM((2, 2, RING, PAD, W), BF16),
            pltpu.VMEM((PAD, W), BF16),
            pltpu.VMEM((PAD, W), BF16),
            pltpu.VMEM((2 * blocks, 2 * blocks), F32),
            pltpu.VMEM((2 * blocks, 2 * blocks), F32),
            pltpu.VMEM((2 * blocks, 2 * blocks), BF16),
            pltpu.VMEM((2 * blocks, E), F32),
            pltpu.VMEM((2 * blocks, E), F32),
            pltpu.VMEM((RING, PAD, E), BF16),
            pltpu.VMEM((2, RING, PAD, E), BF16),
            pltpu.VMEM((2, RING, PAD, E), BF16),
            pltpu.VMEM((RING, PAD, E), BF16),
            pltpu.VMEM((RING, PAD, E), BF16),
            pltpu.VMEM((RING, PAD, E), BF16),
            pltpu.VMEM((RING, PAD, E), BF16),
            pltpu.VMEM((RING, PAD, E), BF16),
            pltpu.VMEM((RING, PAD, E), BF16),
            pltpu.VMEM((3, 8, 128), F32),
            pltpu.VMEM((RING, 8, 128), F32),
            pltpu.VMEM((RING, 8, 128), F32),
            pltpu.VMEM((RING, 8, 128), F32),
            dma((2,)),
            dma((7,)), dma((8,)), dma((7,)), dma((8,)),
            dma((4,)), dma((4,)), dma((3,)), dma((3,)),
            dma((7,)), dma((8,)), dma((7,)), dma((8,)),
            dma((7,)), dma((8,)), dma((7,)), dma((8,)), dma((7,)), dma((8,)),
        ],
        compiler_params=pltpu.CompilerParams(collective_id=0, has_side_effects=True),
    )(ifeat, tfeat, ihead, thead, log_scale.reshape(1), logit_bias.reshape(1), igroup, tgroup)
    return loss[0, 0], gimg, gtxt, gscale[0, 0], gbias[0, 0]


def solution(mesh):
    torus = Mesh(mesh.devices.reshape(8, 8, 4, 2), DEV)
    return jax.shard_map(
        on_device,
        mesh=torus,
        in_specs=(P(DEV, None), P(DEV, None), P(), P(), P(), P(), P(DEV), P(DEV)),
        out_specs=(P(), P(DEV, None), P(DEV, None), P(), P()),
        check_vma=False,
    )
```

time: 273 us -> 57.7 us (0.21)
  blocking collectives: 121 us -> 0 us
  waiting for transfers between devices: 61.6 us -> 0 us
  Pallas kernels: 0 us -> 47.2 us
  local copies, waits for them, and re-layouts: 37.9 us -> 2.77 us
  matrix products: 28.4 us -> 0 us
  between operations: 20.8 us -> 7.25 us
  other arithmetic: 2.83 us -> 0 us
    all_gather x1 -> x0, blocking collectives: 78 us -> none  [on_device(): id_piece = lax.all_gather(stacked_ids, DEV, axis=1, tiled=True)]
    all_gather x1 -> x0, waiting for transfers between devices: 61.6 us -> none  [on_device(): emb_piece = lax.all_gather(stacked_emb, DEV, axis=1, tiled=True)]
    pallas_call x0 -> x1, Pallas kernels: none -> 47.2 us  [on_device(): pl.pallas_call(kernel, out_shape=(one, grad, grad, one, one), in_specs=[v...]
    psum x4 -> x0, blocking collectives: 42.8 us -> none  [one_axis_at_a_time(): x = lax.psum(x, axis)]
    slice x3 -> x0, local copies, waits for them, and re-layouts: 31.4 us -> none  [the longest x1 30.7 us: on_device(): img_piece = emb_piece[0]]
    dot_general x7 -> x0, matrix products: 28.4 us -> none  [the longest x1 13.3 us: on_device(): lax.dot_general(slopes, img_piece, (((0,), (0,)), ((), ())), preferred_el...]
    unnamed x11 -> x2, local copies, waits for them, and re-layouts: 5.9 us -> 2.77 us
  transfers between devices with their start and end apart: 1 -> 0, of which waited for: 1 -> 0; matrix products, arithmetic and copies ran while one was open for 0% -> 0% of each run, Pallas kernels for 0% -> 0%
where the time goes in v1:
time: 57.7 us; the launch traced here: 57.3 us
  Pallas kernels  47.2 us (82%)
  between operations  7.25 us (13%)
  local copies, waits for them, and re-layouts  2.77 us (5%)
    pallas_call x1, Pallas kernels, on_device(): pl.pallas_call(kernel, out_shape=(one, grad, grad, one, one), in_specs=[v...  47.2 us
    unnamed x2, local copies, waits for them, and re-layouts  2.77 us

profile of v1, /device:TPU:1, one launch (start us, length us, event | category | flops | bytes accessed | tf_op | source)
XLA Modules:
  0.0 57.3 jit_solution(6206219994803267464)
XLA Ops:
  1.9 47.2 %shard_map.119 = (f32[1,1]{1,0:T(1,128)}, bf16[12,1152]{1,0:T(8,128)(2,1)}, bf16[12,1152]{1,0:T(8,128)(2,1)}, f32[1,1]{1,0:T(1,128)}, f32[1,1]{1,0:T(1,128)}) custom-call(bf16[12,1152]{1,0:T(8,128)(2,1)} %ifeat.1, bf16[12,1152]{1,0:T(8,128)(2,1)} %tfeat.1, bf16[1152,640]{1,0:T(8,128)(2,1)} %ihead_hbm.1, bf16[1152,640]{1,0:T(8,128)(2,1)} %thead_hbm.1, ...), custom_call_target="tpu_custom_call" | custom-call | tf_op jit(solution)/shard_map/pallas_call | solution.py:273
  49.9 1.4 %copy.21 = bf16[12,1152]{1,0:T(8,128)(2,1)} copy(bf16[12,1152]{1,0:T(8,128)(2,1)} %get-tuple-element.21) | data formatting | bytes 55296
  51.3 1.4 %copy.22 = bf16[12,1152]{1,0:T(8,128)(2,1)} copy(bf16[12,1152]{1,0:T(8,128)(2,1)} %get-tuple-element.22) | data formatting | bytes 55296

commit v2 on v1

v2 whole, which is shorter than its diff:
```python
import functools

import jax
import jax.numpy as jnp
from jax import lax
from jax.experimental import pallas as pl
from jax.experimental.pallas import tpu as pltpu
from jax.sharding import Mesh
from jax.sharding import PartitionSpec as P

DEV = ("dev_0", "dev_1", "dev_2", "dev_3")
RING = 8
ROWS = 12
PAD = 16
D = 1152
E = 640
PAIRS = 6144
NEAR = (4, 3, 5, 2, 6, 1, 7)

EPS = 1e-6
F32 = jnp.float32
BF16 = jnp.bfloat16


def nt(a, b):
    return lax.dot_general(a, b, (((1,), (1,)), ((), ())), preferred_element_type=F32)


def nn(a, b):
    return lax.dot_general(a, b, (((1,), (0,)), ((), ())), preferred_element_type=F32)


def tn(a, b):
    return lax.dot_general(a, b, (((0,), (0,)), ((), ())), preferred_element_type=F32)


def id_features(ids, image_side):
    shape = (PAD, 128)
    row = lax.broadcasted_iota(jnp.int32, shape, 0)
    lane = lax.broadcasted_iota(jnp.int32, shape, 1)
    value = jnp.zeros(shape, jnp.int32)
    for r in range(ROWS):
        value = jnp.where(row == r, ids[r], value)
    high, low = value >> 6, value & 63
    square = high * high + low * low
    upper = jnp.where(row < ROWS, square >> 6, -192)
    lower = square & 63
    one, many = jnp.ones(shape, jnp.int32), jnp.full(shape, 64, jnp.int32)
    if image_side:
        parts = (high, low, upper, lower, many, one)
    else:
        parts = (-2 * high, -2 * low, many, one, upper, lower)
    out = jnp.zeros(shape, jnp.int32)
    for k, part in enumerate(parts):
        out = jnp.where(lane == k, part, out)
    return out.astype(F32).astype(BF16)


def project(feats, head):
    proj = nn(feats[...], head[...])
    length = jnp.sqrt(jnp.sum(proj * proj, axis=1, keepdims=True) + EPS)
    return proj / length, length


def kernel(
    ifeat_hbm, tfeat_hbm, ihead_hbm, thead_hbm, log_scale, logit_bias, igroup_hbm, tgroup_hbm,
    gimg_o, gtxt_o, sums_o,
    igroup, tgroup,
    ifeat, tfeat, ihead, thead, iemb, temb, iid, tid, iown, town, iid_own, tid_own,
    cos_s, dist_s, slope_s, acc_i, acc_t,
    part_i, part_t, core_rx, mid_i, send_t, mid_t, x_rx_i, x_rx_t, ring_i, ring_t,
    sums_v, sum_z, sum_y, sum_c,
    load_sem, s_ring, r_g1i, r_g1t, s_small, r_id, s_x, r_x, s_core, r_core,
    r_r2i, r_r2t, r_r1, r_sum,
):
    z, y, x, c = (lax.axis_index(a) for a in DEV)
    odd = lax.rem(x, 2)
    x_hi = lax.rem(x + 3 + 2 * odd, 4)
    x_lo = x + 1 - 2 * odd
    other = 1 - c

    rz = [lax.rem(z + k, RING) for k in NEAR]
    ry = [lax.rem(y + k, RING) for k in NEAR]
    fz = [lax.rem(z + RING - k, RING) for k in NEAR]
    fy = [lax.rem(y + RING - k, RING) for k in NEAR]
    cluster = [(lax.rem(x + dx, 4), lax.rem(c + dc, 2)) for dx in range(4) for dc in range(2) if (dx, dc) != (0, 0)]

    barrier = pltpu.get_barrier_semaphore()
    for t in rz:
        pl.semaphore_signal(barrier, inc=1, device_id={"dev_0": t})
    for t in ry:
        pl.semaphore_signal(barrier, inc=1, device_id={"dev_1": t})
    for tx, tc in cluster:
        pl.semaphore_signal(barrier, inc=1, device_id={"dev_2": tx, "dev_3": tc})

    loads = [
        pltpu.make_async_copy(a, b, load_sem.at[k])
        for k, (a, b) in enumerate(((ifeat_hbm, ifeat), (ihead_hbm, ihead), (tfeat_hbm, tfeat), (thead_hbm, thead),
                                     (igroup_hbm, igroup), (tgroup_hbm, tgroup)))
    ]
    for copy in loads:
        copy.start()

    def send(src, dst, ssem, rsem, device):
        pltpu.make_async_remote_copy(src, dst, ssem, rsem, device_id=device).start()

    def arrived(dst, rsem):
        pltpu.make_async_copy(dst, dst, rsem).wait()

    for copy in loads[4:]:
        copy.wait()
    iown[...] = jnp.zeros_like(iown)
    town[...] = jnp.zeros_like(town)
    iid_own[...] = id_features(igroup, True)
    tid_own[...] = id_features(tgroup, False)
    iid[0, z] = iid_own[...]
    tid[0, 0, y] = tid_own[...]
    loads[0].wait()
    loads[1].wait()
    img_unit, img_len = project(ifeat, ihead)
    iown[0:ROWS, :] = img_unit.astype(BF16)
    iemb[0, z] = iown[...]
    pl.semaphore_wait(barrier, 21)
    for k, t in enumerate(rz):
        send(iown, iemb.at[0, z], s_ring.at[0], r_g1i.at[z], {"dev_0": t})
    send(iown, iemb.at[1, z], s_x.at[0], r_x.at[0], {"dev_2": x_hi})
    loads[2].wait()
    loads[3].wait()
    txt_unit, txt_len = project(tfeat, thead)
    town[0:ROWS, :] = txt_unit.astype(BF16)
    temb[0, 0, y] = town[...]
    for k, t in enumerate(ry):
        send(town, temb.at[0, 0, y], s_ring.at[1], r_g1t.at[y], {"dev_1": t})
    send(town, temb.at[0, 1, y], s_x.at[1], r_x.at[1], {"dev_2": x_lo})
    for k, t in enumerate(rz):
        send(iid_own, iid.at[0, z], s_small.at[0], r_id.at[0], {"dev_0": t})
    for k, t in enumerate(ry):
        send(tid_own, tid.at[0, 0, y], s_small.at[1], r_id.at[1], {"dev_1": t})

    for k in range(7):
        arrived(iemb.at[0, fz[k]], r_g1i.at[fz[k]])
        send(iemb.at[0, fz[k]], iemb.at[1, fz[k]], s_x.at[0], r_x.at[0], {"dev_2": x_hi})
        arrived(temb.at[0, 0, fy[k]], r_g1t.at[fy[k]])
        send(temb.at[0, 0, fy[k]], temb.at[0, 1, fy[k]], s_x.at[1], r_x.at[1], {"dev_2": x_lo})
    send(temb.at[0, 0], temb.at[1, 0], s_core.at[0], r_core.at[0], {"dev_3": other})
    arrived(iid.at[0, pl.ds(0, 7)], r_id.at[0])
    send(iid.at[0], iid.at[1], s_small.at[2], r_id.at[2], {"dev_2": x_hi})
    arrived(tid.at[0, 0, pl.ds(0, 7)], r_id.at[1])
    send(tid.at[0, 0], tid.at[0, 1], s_small.at[3], r_id.at[3], {"dev_2": x_lo})
    arrived(temb.at[0, 1], r_x.at[1])
    send(temb.at[0, 1], temb.at[1, 1], s_core.at[1], r_core.at[1], {"dev_3": other})
    arrived(tid.at[0, 1], r_id.at[3])
    send(tid.at[0], tid.at[1], s_core.at[3], r_core.at[3], {"dev_3": other})
    arrived(iemb.at[1], r_x.at[0])
    arrived(iid.at[1], r_id.at[2])

    scale_row = jnp.exp(jnp.full((1, 256), log_scale[0], F32))
    bias = logit_bias[0]
    n_img = 2 * RING * PAD

    def pair_block(h, totals):
        ie = iemb[...].reshape(n_img, E)
        te = temb[h].reshape(n_img, E)
        cos_s[...] = nt(ie, te)
        dist_s[...] = nt(iid[...].reshape(n_img, 128), tid[h].reshape(n_img, 128))
        step = 32

        def rows(i, totals):
            at = pl.ds(pl.multiple_of(i * step, step), step)
            cosine = cos_s[at, :]
            dist = dist_s[at, :]
            match = dist < 0.5
            valid = dist > -0.5
            logit = scale_row * cosine + bias
            minus = jnp.where(match, -logit, logit)
            small = jnp.exp(-jnp.abs(minus))
            ratio = 1.0 / (1.0 + small)
            sig = jnp.where(minus >= 0, ratio, small * ratio)
            slope = jnp.where(valid, jnp.where(match, -sig, sig), 0.0)
            soft = jnp.where(valid, jnp.maximum(minus, 0.0) + jnp.log1p(small), 0.0)
            slope_s[at, :] = slope.astype(BF16)
            fold = lambda a: a[0:8] + a[8:16] + a[16:24] + a[24:32]
            return (
                totals[0] + fold(soft),
                totals[1] + fold(slope * cosine),
                totals[2] + fold(slope),
            )

        totals = lax.fori_loop(0, n_img // step, rows, totals)
        slope = slope_s[...]
        return nn(slope, te), tn(slope, ie), totals

    zero = jnp.zeros((8, 256), F32)
    totals = (zero, zero, zero)
    grad_i, grad_t, totals = pair_block(0, totals)
    acc_i[...] = grad_i
    acc_t[...] = grad_t.reshape(2, RING, PAD, E)
    arrived(temb.at[1, 0], r_core.at[0])
    arrived(temb.at[1, 1], r_core.at[1])
    arrived(tid.at[1], r_core.at[3])
    grad_i, grad_t, totals = pair_block(1, totals)
    part_t[...] = grad_t.astype(BF16).reshape(2, RING, PAD, E)
    send(part_t, core_rx, s_core.at[2], r_core.at[2], {"dev_3": other})
    lanes = [t[:, 0:128] + t[:, 128:256] for t in totals]
    mine = jnp.concatenate([jnp.sum(t, axis=0, keepdims=True) for t in lanes] + [jnp.zeros((5, 128), F32)], axis=0)
    sums_v[0] = mine
    sum_c[2 * x + c] = mine
    for k, (tx, tc) in enumerate(cluster):
        send(sums_v.at[0], sum_c.at[2 * x + c], s_small.at[4], r_sum.at[0], {"dev_2": tx, "dev_3": tc})
    grad_i = (grad_i + acc_i[...]).reshape(2, RING, PAD, E)
    part_i[...] = grad_i[1].astype(BF16)
    acc_i[...] = grad_i.reshape(n_img, E)
    order_z = rz + [z]
    order_y = ry + [y]
    for k, t in enumerate(order_z):
        send(part_i.at[t], x_rx_i.at[t], s_x.at[2], r_r2i.at[t], {"dev_2": x_hi})

    arrived(core_rx, r_core.at[2])
    grad_t = acc_t[...] + core_rx[...].astype(F32)
    send_t[...] = grad_t[1].astype(BF16)
    acc_t[0] = grad_t[0]
    for k, t in enumerate(order_y):
        send(send_t.at[t], x_rx_t.at[t], s_x.at[3], r_r2t.at[t], {"dev_2": x_lo})

    arrived(sum_c.at[pl.ds(0, 7)], r_sum.at[0])
    mine = functools.reduce(lambda a, b: a + b, [sum_c[k] for k in range(8)])
    sums_v[1] = mine
    sum_z[z] = mine
    for k, t in enumerate(rz):
        send(sums_v.at[1], sum_z.at[z], s_small.at[5], r_sum.at[1], {"dev_0": t})

    for k, t in enumerate(order_z):
        arrived(x_rx_i.at[t], r_r2i.at[t])
        at = pl.ds(pl.multiple_of(t * PAD, PAD), PAD)
        block = (acc_i[at, :] + x_rx_i[t].astype(F32)).astype(BF16)
        if k < 7:
            mid_i[t] = block
            send(mid_i.at[t], ring_i.at[z], s_ring.at[2], r_r1.at[0], {"dev_0": t})
        else:
            ring_i[z] = block
    for k, t in enumerate(order_y):
        arrived(x_rx_t.at[t], r_r2t.at[t])
        block = (acc_t[0, t] + x_rx_t[t].astype(F32)).astype(BF16)
        if k < 7:
            mid_t[t] = block
            send(mid_t.at[t], ring_t.at[y], s_ring.at[3], r_r1.at[1], {"dev_1": t})
        else:
            ring_t[y] = block

    arrived(sum_z.at[pl.ds(0, 7)], r_sum.at[1])
    mine = functools.reduce(lambda a, b: a + b, [sum_z[k] for k in range(RING)])
    sums_v[2] = mine
    sum_y[y] = mine
    for k, t in enumerate(ry):
        send(sums_v.at[2], sum_y.at[y], s_small.at[6], r_sum.at[2], {"dev_1": t})

    scale_e = jnp.exp(jnp.full((1, E), log_scale[0], F32))

    def backward(ring, unit, length, head, out):
        grad = functools.reduce(lambda a, b: a + b, [ring[k].astype(F32) for k in range(RING)])
        grad = scale_e * grad[0:ROWS]
        inner = jnp.sum(unit * grad, axis=1, keepdims=True)
        low = ((grad - unit * inner) / length).astype(BF16)
        out[...] = nt(low, head[...]).astype(BF16)

    arrived(ring_i.at[pl.ds(0, 7)], r_r1.at[0])
    backward(ring_i, img_unit, img_len, ihead, gimg_o)
    arrived(ring_t.at[pl.ds(0, 7)], r_r1.at[1])
    backward(ring_t, txt_unit, txt_len, thead, gtxt_o)

    arrived(sum_y.at[pl.ds(0, 7)], r_sum.at[2])
    total = functools.reduce(lambda a, b: a + b, [sum_y[k] for k in range(RING)])
    row = lax.broadcasted_iota(jnp.int32, (8, 128), 0)
    sums_o[...] = total * jnp.where(row == 1, jnp.exp(jnp.full((8, 128), log_scale[0], F32)), 1.0)

    seven = pl.ds(0, 7)
    arrived(iemb.at[0, seven], s_ring.at[0])
    arrived(temb.at[0, 0, seven], s_ring.at[1])
    arrived(mid_i.at[seven], s_ring.at[2])
    arrived(mid_t.at[seven], s_ring.at[3])
    arrived(iid.at[0, seven], s_small.at[0])
    arrived(tid.at[0, 0, seven], s_small.at[1])
    arrived(iid.at[0], s_small.at[2])
    arrived(tid.at[0, 0], s_small.at[3])
    for k, part in enumerate((sum_c, sum_z, sum_y)):
        arrived(part.at[seven], s_small.at[4 + k])
    arrived(iemb.at[0], s_x.at[0])
    arrived(temb.at[0, 0], s_x.at[1])
    arrived(part_i, s_x.at[2])
    arrived(send_t, s_x.at[3])
    arrived(temb.at[0, 0], s_core.at[0])
    arrived(temb.at[0, 1], s_core.at[1])
    arrived(part_t, s_core.at[2])
    arrived(tid.at[0], s_core.at[3])


def finish(gimg, gtxt, sums, loss_o, gimg_o, gtxt_o, gscale_o, gbias_o):
    gimg_o[...] = gimg[...]
    gtxt_o[...] = gtxt[...]
    whole = jnp.sum(sums[...], axis=1, keepdims=True) / PAIRS
    loss_o[...] = whole[0:1]
    gscale_o[...] = whole[1:2]
    gbias_o[...] = whole[2:3]


def on_device(ifeat, tfeat, ihead, thead, log_scale, logit_bias, igroup, tgroup):
    vmem = pl.BlockSpec(memory_space=pltpu.VMEM)
    smem = pl.BlockSpec(memory_space=pltpu.SMEM)
    hbm = pl.BlockSpec(memory_space=pltpu.HBM)
    dma = pltpu.SemaphoreType.DMA
    blocks = RING * PAD
    one = jax.ShapeDtypeStruct((1, 1), F32)
    grad = jax.ShapeDtypeStruct((ROWS, D), BF16)
    ring = pltpu.VMEM((RING, PAD, E), BF16)
    two_rings = pltpu.VMEM((2, RING, PAD, E), BF16)
    small = pltpu.VMEM((RING, 8, 128), F32)
    arrays = (ifeat, tfeat, ihead, thead, igroup, tgroup)
    ifeat, tfeat, ihead, thead, igroup, tgroup = [pltpu.with_memory_space_constraint(a, pltpu.HBM) for a in arrays]
    gimg, gtxt, sums = pl.pallas_call(
        kernel,
        out_shape=(grad, grad, jax.ShapeDtypeStruct((8, 128), F32)),
        in_specs=[hbm, hbm, hbm, hbm, smem, smem, hbm, hbm],
        out_specs=[vmem] * 3,
        scratch_shapes=[
            pltpu.SMEM((ROWS,), jnp.int32),
            pltpu.SMEM((ROWS,), jnp.int32),
            pltpu.VMEM((ROWS, D), BF16),
            pltpu.VMEM((ROWS, D), BF16),
            pltpu.VMEM((D, E), BF16),
            pltpu.VMEM((D, E), BF16),
            two_rings,
            pltpu.VMEM((2, 2, RING, PAD, E), BF16),
            pltpu.VMEM((2, RING, PAD, 128), BF16),
            pltpu.VMEM((2, 2, RING, PAD, 128), BF16),
            pltpu.VMEM((PAD, E), BF16),
            pltpu.VMEM((PAD, E), BF16),
            pltpu.VMEM((PAD, 128), BF16),
            pltpu.VMEM((PAD, 128), BF16),
            pltpu.VMEM((2 * blocks, 2 * blocks), F32),
            pltpu.VMEM((2 * blocks, 2 * blocks), F32),
            pltpu.VMEM((2 * blocks, 2 * blocks), BF16),
            pltpu.VMEM((2 * blocks, E), F32),
            pltpu.VMEM((2, RING, PAD, E), F32),
            ring, two_rings, two_rings, ring, ring, ring, ring, ring, ring, ring,
            pltpu.VMEM((3, 8, 128), F32),
            small, small, small,
            dma((6,)), dma((4,)), dma((8,)), dma((8,)), dma((7,)), dma((4,)), dma((4,)), dma((2,)), dma((4,)), dma((4,)),
            dma((8,)), dma((8,)), dma((2,)), dma((3,)),
        ],
        compiler_params=pltpu.CompilerParams(
            collective_id=0, has_side_effects=True, vmem_limit_bytes=24 << 20
        ),
    )(ifeat, tfeat, ihead, thead, log_scale.reshape(1), logit_bias.reshape(1), igroup, tgroup)
    loss, gimg, gtxt, gscale, gbias = pl.pallas_call(
        finish,
        out_shape=(one, grad, grad, one, one),
        in_specs=[vmem] * 3,
        out_specs=[vmem] * 5,
        compiler_params=pltpu.CompilerParams(vmem_limit_bytes=4 << 20),
    )(gimg, gtxt, sums)
    return loss[0, 0], gimg, gtxt, gscale[0, 0], gbias[0, 0]


def solution(mesh):
    torus = Mesh(mesh.devices.reshape(8, 8, 4, 2), DEV)
    return jax.shard_map(
        on_device,
        mesh=torus,
        in_specs=(P(DEV, None), P(DEV, None), P(), P(), P(), P(), P(DEV), P(DEV)),
        out_specs=(P(), P(DEV, None), P(DEV, None), P(), P()),
        check_vma=False,
    )
```

time: 57.7 us -> 43.8 us (0.76)
  Pallas kernels: 47.2 us -> 41.7 us
  between operations: 7.25 us -> 1.93 us
  local copies, waits for them, and re-layouts: 2.77 us -> 0 us
    pallas_call x1 -> x2, Pallas kernels: 47.2 us -> 41.7 us  [the longest x1 41.1 us: on_device(): pl.pallas_call(kernel, out_shape=(grad, grad, jax.ShapeDtypeStruct((8, 12...]
    unnamed x2 -> x0, local copies, waits for them, and re-layouts: 2.77 us -> none
where the time goes in v2:
time: 43.8 us; the launch traced here: 43.6 us
  Pallas kernels  41.7 us (95%)
  between operations  1.93 us (4%)
    pallas_call x1, Pallas kernels, on_device(): pl.pallas_call(kernel, out_shape=(grad, grad, jax.ShapeDtypeStruct((8, 12...  41.1 us

profile of v2, /device:TPU:1, one launch (start us, length us, event | category | flops | bytes accessed | tf_op | source)
XLA Modules:
  0.0 43.6 jit_solution(10209707168758506330)
XLA Ops:
  1.9 41.1 %shard_map.119 = (bf16[12,1152]{1,0:T(8,128)(2,1)S(1)}, bf16[12,1152]{1,0:T(8,128)(2,1)S(1)}, f32[8,128]{1,0:T(8,128)S(1)}) custom-call(bf16[12,1152]{1,0:T(8,128)(2,1)} %ifeat_hbm.1, bf16[12,1152]{1,0:T(8,128)(2,1)} %tfeat_hbm.1, bf16[1152,640]{1,0:T(8,128)(2,1)} %ihead_hbm.1, bf16[1152,640]{1,0:T(8,128)(2,1)} %thead_hbm.1, f32[1]{0:T(128)} %bitcast.5.log_scale, ...), custom_call_target="tpu_custom_call" | custom-call | tf_op jit(solution)/shard_map/pallas_call | solution.py:319
  43.0 0.6 %shard_map.120 = (f32[1,1]{1,0:T(1,128)}, bf16[12,1152]{1,0:T(8,128)(2,1)}, bf16[12,1152]{1,0:T(8,128)(2,1)}, f32[1,1]{1,0:T(1,128)}, f32[1,1]{1,0:T(1,128)}) custom-call(bf16[12,1152]{1,0:T(8,128)(2,1)S(1)} %get-tuple-element.13.gimg, bf16[12,1152]{1,0:T(8,128)(2,1)S(1)} %get-tuple-element.14.gtxt, f32[8,128]{1,0:T(8,128)S(1)} %get-tuple-element.15.sums), custom_call_target="tpu_custom_call" | custom-call | tf_op jit(solution)/shard_map/pallas_call | solution.py:354
